TPU v7x, 32 devices: a whole 2x2x4 slice. The times are simulated.
32 devices in a mesh: sample: 8 (over y, x, core), line: 4 (over z).
Axes of the slice: x: 2, y: 2, z: 4, core: 2. Of those that a mesh axis runs over, the one named last changes fastest.
Arguments:
- wind_dev: bfloat16 [4096, 10000], P('sample', 'line'), may hold values from -6 to 6
- ptdf: bfloat16 [4096, 10000], P('line'), may hold values from -0.0625 to 0.0625
- region_weights: bfloat16 [31, 10000], replicated, may hold values from -0.0625 to 0.0625
- incidence: int32 [12706, 2], replicated, may hold values from 0 to 9999
- monitored: int32 [4096], P('line'), may hold values from 0 to 12705
- ratings: float32 [12706], replicated, may hold values from 1 to 3
- base_flow: float32 [4096], P('line'), may hold values from -6 to 6
- line_cost: float32 [4096], P('line'), may hold values from 0.2 to 20
- policy: float32 [32, 4096], P(None, 'line'), may hold values from -0.6 to 0.6
Outputs:
- new_policy: float32 [32, 4096], P(None, 'line')
- new_flows: float32 [4096, 4096], P('sample', 'line')
- decrement: float32 [], replicated
- grad_norm: float32 [], replicated
All inputs are finite; a program needn't handle non-finite values.
Results may differ from a plain program's by a relative error of at most 0.0003.
Values may be sent and summed in bfloat16 or wider, within the bound.
A program may use at most 128 MiB of HBM per device.

v0:
```python
import jax
import jax.numpy as jnp
from jax import lax
from jax.sharding import PartitionSpec as P

ridge_weight = 1.0
barrier_weight = 0.1
smoothing = 0.5


def penalty_terms(factors, ends_diff, slope_term, curve_term, weight):
    highest = lax.Precision.HIGHEST
    regions = factors.shape[1]
    lines_here = slope_term.shape[1]
    outer_prod = (factors[:, :, None] * factors[:, None, :]).reshape(
        factors.shape[0], regions * regions
    )
    block_rr = lax.dot_general(outer_prod, curve_term, (((0,), (0,)), ((), ())), precision=highest)
    weighted = curve_term * ends_diff
    cross_re = lax.dot_general(factors, weighted, (((0,), (0,)), ((), ())), precision=highest)
    corner = jnp.sum(weighted * ends_diff, axis=0)
    upper_rows = jnp.concatenate(
        [block_rr.reshape(regions, regions, lines_here), cross_re[:, None, :]], axis=1
    )
    bottom = jnp.concatenate([cross_re[None, :, :], corner[None, None, :]], axis=1)
    hessian = jnp.concatenate([upper_rows, bottom], axis=0) * weight
    grad_rr = lax.dot_general(factors, slope_term, (((0,), (0,)), ((), ())), precision=highest)
    gradient = (
        jnp.concatenate([grad_rr, jnp.sum(slope_term * ends_diff, axis=0)[None, :]], axis=0)
        * weight
    )
    return (hessian.reshape((regions + 1) * (regions + 1), lines_here), gradient)


def factor_solve(hessian, gradient):
    features = gradient.shape[0]
    positions = jnp.arange(features, dtype=jnp.int32)

    def chol_column(column, lower_tri):
        target = lax.dynamic_index_in_dim(hessian, column, 1, keepdims=False)
        row_here = lax.dynamic_index_in_dim(lower_tri, column, 0, keepdims=False)
        running = target - jnp.sum(lower_tri * row_here[None, :, :], axis=1)
        pivot_val = jnp.sqrt(lax.dynamic_index_in_dim(running, column, 0, keepdims=False))
        new_col = jnp.where(
            (positions >= column)[:, None], running / pivot_val[None, :], jnp.zeros_like(running)
        )
        select = (positions == column).astype(hessian.dtype)
        return lower_tri + new_col[:, None, :] * select[None, :, None]

    lower_tri = lax.fori_loop(0, features, chol_column, jnp.zeros_like(hessian))

    def forward_row(row_index, forward):
        row_here = lax.dynamic_index_in_dim(lower_tri, row_index, 0, keepdims=False)
        running = lax.dynamic_index_in_dim(gradient, row_index, 0, keepdims=False) - jnp.sum(
            row_here * forward, axis=0
        )
        value = running / lax.dynamic_index_in_dim(row_here, row_index, 0, keepdims=False)
        select = (positions == row_index).astype(gradient.dtype)
        return forward + select[:, None] * value[None, :]

    forward = lax.fori_loop(0, features, forward_row, jnp.zeros_like(gradient))

    def backward_row(turn, backward):
        row_index = features - 1 - turn
        col_here = lax.dynamic_index_in_dim(lower_tri, row_index, 1, keepdims=False)
        running = lax.dynamic_index_in_dim(forward, row_index, 0, keepdims=False) - jnp.sum(
            col_here * backward, axis=0
        )
        value = running / lax.dynamic_index_in_dim(col_here, row_index, 0, keepdims=False)
        select = (positions == row_index).astype(gradient.dtype)
        return backward + select[:, None] * value[None, :]

    backward = lax.fori_loop(0, features, backward_row, jnp.zeros_like(gradient))
    return (forward, -backward)


def owner_step(hessian_flat, gradient, policy_part):
    features = gradient.shape[0]
    lines_here = gradient.shape[1]
    hessian = hessian_flat.reshape(features, features, lines_here)
    margin_sq = 1.0 - policy_part * policy_part
    diag_terms = ridge_weight + barrier_weight * 2.0 * (1.0 + policy_part * policy_part) / (
        margin_sq * margin_sq
    )
    hessian = hessian + jnp.eye(features, dtype=hessian.dtype)[:, :, None] * diag_terms[:, None, :]
    gradient = (
        gradient + ridge_weight * policy_part + barrier_weight * 2.0 * policy_part / margin_sq
    )
    forward, newton_step = factor_solve(hessian, gradient)
    return (gradient, forward, newton_step)


def shards(
    wind_dev, ptdf, region_weights, incidence, monitored, ratings, base_flow, line_cost, policy
):
    highest = lax.Precision.HIGHEST
    regions = region_weights.shape[0]
    endpoints = jnp.take(incidence, monitored, axis=0)
    from_bus = endpoints[:, 0]
    to_bus = endpoints[:, 1]
    rating = jnp.take(ratings, monitored)
    scen_here = wind_dev.shape[0]
    lines_here = ptdf.shape[0]

    def pick_buses(wind_piece, bus_ids):
        piece_width = wind_piece.shape[1]
        inside = (bus_ids >= 0) & (bus_ids < piece_width)
        picked = jnp.take(wind_piece, jnp.clip(bus_ids, 0, piece_width - 1), axis=1).astype(
            jnp.float32
        )
        return jnp.where(inside[None, :], picked, 0.0)

    wind_piece = lax.all_gather(wind_dev, "line", axis=1, tiled=True)
    grid_flow = lax.dot_general(
        wind_piece, ptdf, (((1,), (1,)), ((), ())), preferred_element_type=jnp.float32
    )
    ends_diff = pick_buses(wind_piece, to_bus) - pick_buses(wind_piece, from_bus)
    grid_flow, ends_diff = (grid_flow, ends_diff)
    factors = lax.dot_general(
        wind_piece, region_weights, (((1,), (1,)), ((), ())), preferred_element_type=jnp.float32
    )
    grid_flow, ends_diff, folded_factors = (grid_flow, ends_diff, factors)
    factors = folded_factors
    line_flow = (
        grid_flow
        + base_flow[None, :]
        + jnp.dot(factors, policy[:regions], precision=highest)
        + policy[regions][None, :] * ends_diff
    )
    prob_up = jax.nn.sigmoid((line_flow - rating[None, :]) / smoothing)
    prob_down = jax.nn.sigmoid((-line_flow - rating[None, :]) / smoothing)
    slope_term = prob_up - prob_down
    curve_term = (prob_up * (1.0 - prob_up) + prob_down * (1.0 - prob_down)) / smoothing
    weight = line_cost / (scen_here * lax.axis_size("sample"))
    hessian_part, gradient_part = penalty_terms(factors, ends_diff, slope_term, curve_term, weight)
    hessian_sum, gradient_sum = (
        lax.psum_scatter(hessian_part, "sample", scatter_dimension=1, tiled=True),
        lax.psum_scatter(gradient_part, "sample", scatter_dimension=1, tiled=True),
    )
    share_width = gradient_sum.shape[1]
    policy_share = lax.dynamic_slice_in_dim(
        policy, lax.axis_index("sample") * share_width, share_width, 1
    )
    gradient, forward, newton_step = owner_step(hessian_sum, gradient_sum, policy_share)
    decrement_sq, norm_sq = lax.psum(
        (jnp.sum(forward * forward), jnp.sum(gradient * gradient)), ("sample", "line")
    )
    full_step = lax.all_gather(newton_step, "sample", axis=1, tiled=True)
    total_lines = lines_here * lax.axis_size("line")
    features = policy.shape[0]
    step_length = 1.0 / (1.0 + jnp.sqrt(decrement_sq / (barrier_weight * features * total_lines)))
    new_policy = policy + step_length * full_step
    shift_flow = (
        jnp.dot(factors, full_step[:regions], precision=highest)
        + full_step[regions][None, :] * ends_diff
    )
    new_flows = line_flow + step_length * shift_flow
    return (new_policy, new_flows, jnp.sqrt(decrement_sq), jnp.sqrt(norm_sq))


def solution(mesh):
    placed = (
        P("sample", "line"),
        P("line", None),
        P(),
        P(),
        P("line"),
        P(),
        P("line"),
        P("line"),
        P(None, "line"),
    )
    return jax.shard_map(
        shards,
        mesh=mesh,
        in_specs=placed,
        out_specs=(P(None, "line"), P("sample", "line"), P(), P()),
        check_vma=False,
    )
```

profile of v0, /device:TPU:0, one launch (start us, length us, event | category | flops | bytes accessed | tf_op | source)
XLA Modules:
  0.0 437.1 jit_solution(4000536996957943662)
XLA Ops:
  7.2 0.7 all-gather.3.cloned.1.call-update
  8.0 0.2 copy-done.8
  8.1 4.1 copy.20
  12.3 5.7 %gather_fusion = s32[1024,2]{1,0:T(8,128)S(1)} fusion(s32[12706,2]{1,0:T(8,128)} %copy.20, s32[1024]{0:T(1024)S(1)} %fusion.32), kind=kCustom, calls=%fused_computation.2 | custom fusion | bytes 20480 | tf_op jit(solution)/shard_map/jit(_take)/gather | solution.py:98
  18.0 6.2 %gather_fusion.1 = f32[1024]{0:T(1024)S(1)} fusion(f32[12706]{0:T(1024)S(1)} %copy-done.2, s32[1024]{0:T(1024)S(1)} %fusion.32), kind=kCustom, calls=%fused_computation.3 | custom fusion | bytes 12288 | tf_op jit(solution)/shard_map/jit(_take)/gather | solution.py:101
  24.2 0.2 broadcast_select_fusion.1
  24.4 0.5 clamp_reduce_fusion.1
  24.9 0.5 and_reduce_fusion.1
  25.5 167.0 %all-gather.3.cloned.1.call-done = bf16[4,2500,512]{2,1,0:T(8,128)(2,1)} async-done(((bf16[1,2500,512]{2,1,0:T(8,128)(2,1)}), bf16[4,2500,512]{2,1,0:T(8,128)(2,1)}) %all-gather.3.cloned.1.call-update) | async-done | bytes 10240016 | tf_op jit(solution)/shard_map/all_gather | solution.py:113
  192.5 11.5 %reshape.198 = bf16[10000,512]{1,0:T(8,128)(2,1)} reshape(bf16[4,2500,512]{2,1,0:T(8,128)(2,1)} %all-gather.3.cloned.1.call-done) | data formatting | bytes 20480000
  203.9 9.2 %gather_fusion.3 = bf16[1024,512]{1,0:T(8,128)(2,1)S(1)} fusion(bf16[512,10000]{0,1:T(8,128)(2,1)} %bitcast.127, s32[1024]{0:T(1024)S(1)} %get-tuple-element.496), kind=kCustom, calls=%fused_computation.1.clone | custom fusion | bytes 2101248 | tf_op jit(solution)/shard_map/jit(_take)/gather | solution.py:108
  213.2 0.5 copy.22
  213.7 9.6 %gather_fusion.2 = bf16[1024,512]{1,0:T(8,128)(2,1)S(1)} fusion(bf16[512,10000]{0,1:T(8,128)(2,1)} %bitcast.128, s32[1024]{0:T(1024)S(1)} %get-tuple-element.495), kind=kCustom, calls=%fused_computation.clone | custom fusion | bytes 2101248 | tf_op jit(solution)/shard_map/jit(_take)/gather | solution.py:108
  223.3 1.3 copy.21
  224.7 5.7 %fusion.37 = f32[512,31]{0,1:T(8,128)S(1)} fusion(bf16[10000,512]{1,0:T(8,128)(2,1)} %reshape.198, bf16[31,10000]{1,0:T(8,128)(2,1)S(1)} %copy-done), kind=kOutput, calls=%fused_computation.90 | convolution fusion | flops 317440000 | bytes 10923488 | tf_op jit(solution)/shard_map/dot_general | solution.py:119
  230.3 17.1 %fusion.38 = f32[512,1024]{1,0:T(8,128)S(1)} fusion(bf16[10000,512]{1,0:T(8,128)(2,1)} %reshape.198, bf16[1024,10000]{0,1:T(8,128)(2,1)} %param.18), kind=kOutput, calls=%fused_computation.91 | convolution fusion | flops 10485760000 | bytes 32817152 | tf_op jit(solution)/shard_map/dot_general | solution.py:114
  247.5 4.3 multiply_reduce_fusion.2
  251.8 2.2 fusion.27
  254.0 3.3 fusion.25
  257.3 0.2 broadcast_multiply_fusion
  257.5 0.7 maximum_multiply_fusion
  258.4 1.5 mul.325
  259.9 1.7 dot_general.30
  261.6 9.4 %fusion.23 = f32[31,31,1024]{2,1,0:T(8,128)S(1)} fusion(f32[31,31,512]{2,1,0:T(8,128)S(1)} %dot_general.30, f32[512,1024]{1,0:T(8,128)} %copy-done.12, f32[1024]{0:T(1024)S(1)} %get-tuple-element.487), kind=kOutput, calls=%fused_computation.49 | convolution fusion | flops 6055002112 | bytes 8005632 | tf_op jit(solution)/shard_map/dot_general | solution.py:18
  271.0 0.9 maximum_maximum_fusion
  271.9 2.4 bitcast_multiply_fusion.1
  274.4 15.7 %reduce-scatter.3.cloned.1.call-done = f32[32,128]{1,0:T(8,128)} async-done(((f32[32,1024]{1,0:T(8,128)}), f32[32,128]{1,0:T(8,128)}) %reduce-scatter.3.cloned.1.call-update) | async-done | bytes 16400 | tf_op jit(solution)/shard_map/reduce_scatter | solution.py:138
  290.1 1.3 multiply_reduce_fusion.4
  291.5 53.1 %reduce-scatter.5.cloned.1.call-done = f32[1024,128]{1,0:T(8,128)} async-done(((f32[1024,1024]{1,0:T(8,128)}), f32[1024,128]{1,0:T(8,128)}) %reduce-scatter.5.cloned.1.call-update) | async-done | bytes 524304 | tf_op jit(solution)/shard_map/reduce_scatter | solution.py:137
  344.6 1.2 multiply_add_fusion.5
  345.8 15.0 %while.51 = (s32[]{:T(128)}, f32[32,32,128]{2,1,0:T(8,128)S(1)}, f32[32,32,128]{2,1,0:T(8,128)S(1)}, s32[]{:T(128)}, s32[]{:T(128)}) while((s32[]{:T(128)}, f32[32,32,128]{2,1,0:T(8,128)S(1)}, f32[32,32,128]{2,1,0:T(8,128)S(1)}, s32[]{:T(128)}, s32[]{:T(128)}) %tuple.130), condition=%wide.region_4.6_spmd.clone.clone, body=%wide.region_2.5_spmd.clone.clone.sunk | while | flops 925923 | bytes 2787745 | solution.py:50
  346.2 0.1 multiply_add_fusion.12
  346.6 0.1 multiply_add_fusion.12
  347.1 0.1 multiply_add_fusion.12
  347.6 0.1 multiply_add_fusion.12
  348.0 0.1 multiply_add_fusion.12
  348.5 0.1 multiply_add_fusion.12
  349.0 0.1 multiply_add_fusion.12
  349.4 0.1 multiply_add_fusion.12
  349.9 0.1 multiply_add_fusion.12
  350.4 0.1 multiply_add_fusion.12
  350.9 0.1 multiply_add_fusion.12
  351.3 0.1 multiply_add_fusion.12
  351.8 0.1 multiply_add_fusion.12
  352.3 0.1 multiply_add_fusion.12
  352.7 0.1 multiply_add_fusion.12
  353.2 0.1 multiply_add_fusion.12
  353.7 0.1 multiply_add_fusion.12
  354.1 0.1 multiply_add_fusion.12
  354.6 0.1 multiply_add_fusion.12
  355.1 0.1 multiply_add_fusion.12
  355.6 0.1 multiply_add_fusion.12
  356.5 0.1 multiply_add_fusion.12
  357.0 0.1 multiply_add_fusion.12
  357.9 0.1 multiply_add_fusion.12
  358.4 0.1 multiply_add_fusion.12
  359.8 0.1 multiply_add_fusion.12
  360.9 4.2 while.49
  365.1 0.6 multiply_reduce_fusion.5
  365.7 5.2 %while.50 = (s32[]{:T(128)}, f32[32,128]{1,0:T(8,128)S(1)}, f32[32,128]{1,0:T(8,128)S(1)}, f32[32,32,128]{2,1,0:T(8,128)S(1)}, s32[]{:T(128)}, /*index=5*/s32[]{:T(128)}, s32[]{:T(128)}, s32[]{:T(128)}) while((s32[]{:T(128)}, f32[32,128]{1,0:T(8,128)S(1)}, f32[32,128]{1,0:T(8,128)S(1)}, f32[32,32,128]{2,1,0:T(8,128)S(1)}, ...), condition=%wide.region_14.16_spmd.clone, body=%wide.region_12.15_spmd.clone.sunk | while | flops 24776 | bytes 101814 | solution.py:73
  370.9 9.3 %all_gather.7 = f32[32,1024]{1,0:T(8,128)S(1)} all-gather(f32[32,128]{1,0:T(8,128)S(1)} %neg.15), channel_id=1, replica_groups=mesh['sample'=8,'line'=4] {'sample'}, dimensions={1}, use_global_device_ids=true | all-gather | bytes 147456 | tf_op jit(solution)/shard_map/all_gather | solution.py:148
  380.1 39.8 %all-reduce = (f32[]{:T(128)}, f32[]{:T(128)}) all-reduce(f32[]{:T(128)} %multiply_reduce_fusion.5, f32[]{:T(128)} %get-tuple-element.485), channel_id=1, replica_groups=mesh['sample'=8,'line'=4] {'sample','line'}, use_global_device_ids=true, to_apply=%region_11.13 | all-reduce | flops 2 | bytes 16 | tf_op jit(solution)/shard_map/psum | solution.py:145
  421.3 0.7 multiply_add_fusion.6
  422.0 5.5 %multiply_add_fusion.3 = f32[512,1024]{1,0:T(8,128)} fusion(f32[512,1024]{1,0:T(8,128)} %copy-done.12, f32[512,31]{0,1:T(8,128)S(1)} %fusion.37, f32[1024]{0:T(1024)S(1)} %bitcast.139, f32[]{:T(128)S(6)} %div.86, f32[32,1024]{1,0:T(8,128)S(1)} %all_gather.7, bf16[1024,512]{0,1:T(8,128)(2,1)S(1)} %copy-done.4, pred[1024]{0:T(1024)(128)(4,1)S(1)} %get-tuple-element.493, ...), kind=kOutput, calls=%fused_computation.51 | convolution fusion | flops 200802304 | bytes 6494212 | tf_op jit(solution)/shard_map/dot_general | solution.py:154
  (561 shorter events, 17.9 us)
Async XLA Ops:
  7.2 217.5 %copy-start = (bf16[31,10000]{1,0:T(8,128)(2,1)S(1)}, bf16[31,10000]{1,0:T(8,128)(2,1)}, u32[]{:S(2)}) copy-start(bf16[31,10000]{1,0:T(8,128)(2,1)} %param.19) | copy-start | bytes 1860004
  7.2 1.0 copy-start.8
  7.2 185.3 %all-gather.3.cloned.1.call-start = ((), (), s32[]{:S(2)}) async-start(), calls=%async_computation.4 | async-start | bytes 12820480 | tf_op jit(solution)/shard_map/all_gather | solution.py:113
  7.9 4.3 copy-start.9
  7.9 282.2 %reduce-scatter.3.cloned.1.call-start = ((), (), s32[]{:S(2)}) async-start(), calls=%async_computation.2 | async-start | bytes 147456 | tf_op jit(solution)/shard_map/reduce_scatter | solution.py:138
  12.3 5.7 %copy-start.2 = (f32[12706]{0:T(1024)S(1)}, f32[12706]{0:T(1024)}, u32[]{:S(2)}) copy-start(f32[12706]{0:T(1024)} %param.22) | copy-start | bytes 152476
  18.0 6.2 %copy-start.7 = (f32[32,1024]{1,0:T(8,128)S(1)}, f32[32,1024]{1,0:T(8,128)}, u32[]{:S(2)}) copy-start(f32[32,1024]{1,0:T(8,128)} %param.25) | copy-start | bytes 393220
  24.1 1.3 copy-start.10
  213.7 40.3 %copy-start.3 = (bf16[1024,512]{0,1:T(8,128)(2,1)}, bf16[1024,512]{0,1:T(8,128)(2,1)S(1)}, u32[]{:S(2)}) copy-start(bf16[1024,512]{0,1:T(8,128)(2,1)S(1)} %copy.22) | copy-start | bytes 3145732
  230.3 17.1 %copy-start.5 = (bf16[1024,512]{0,1:T(8,128)(2,1)S(1)}, bf16[1024,512]{0,1:T(8,128)(2,1)}, u32[]{:S(2)}) copy-start(bf16[1024,512]{0,1:T(8,128)(2,1)} %copy.21) | copy-start | bytes 3145732
  230.3 17.1 %copy-start.11 = (f32[1024]{0:T(1024)S(1)}, f32[1024]{0:T(1024)}, u32[]{:S(2)}) copy-start(f32[1024]{0:T(1024)} %param.23) | copy-start | bytes 12292
  251.8 2.2 copy-start.12
  258.2 86.3 %reduce-scatter.5.cloned.1.call-start = ((), (), s32[]{:S(2)}) async-start(), calls=%async_computation.3 | async-start | bytes 4718592 | tf_op jit(solution)/shard_map/reduce_scatter | solution.py:137
  345.8 76.2 %copy-start.4 = (bf16[1024,512]{0,1:T(8,128)(2,1)S(1)}, bf16[1024,512]{0,1:T(8,128)(2,1)}, u32[]{:S(2)}) copy-start(bf16[1024,512]{0,1:T(8,128)(2,1)} %copy-done.3) | copy-start | bytes 3145732
  345.8 76.2 %copy-start.6 = (bf16[1024,512]{0,1:T(8,128)(2,1)S(1)}, bf16[1024,512]{0,1:T(8,128)(2,1)}, u32[]{:S(2)}) copy-start(bf16[1024,512]{0,1:T(8,128)(2,1)} %copy.21) | copy-start | bytes 3145732
  422.0 6.3 %copy-start.1 = (bf16[31,10000]{1,0:T(8,128)(2,1)S(1)}, bf16[31,10000]{1,0:T(8,128)(2,1)}, u32[]{:S(2)}) copy-start(bf16[31,10000]{1,0:T(8,128)(2,1)} %param.19) | copy-start | bytes 1860004
Sparse Core Ops, SparseCore 0:
  9.6 182.8 all-gather.2
  258.4 31.7 reduce-scatter.2
  293.5 51.0 reduce-scatter.4
where the time goes:
time: 438 us; the launch traced here: 437 us
  waiting for transfers between devices  237 us (54%)
  local copies, waits for them, and re-layouts  53.6 us (12%)
  blocking collectives  49 us (11%)
  matrix products  47.4 us (11%)
  other arithmetic  28.4 us (6%)
  between operations  18.5 us (4%)
    all_gather x1, waiting for transfers between devices, shards(): wind_piece = lax.all_gather(wind_dev, 'line', axis=1, tiled=True)  167 us
    reduce_scatter x1, waiting for transfers between devices, shards(): lax.psum_scatter(hessian_part, 'sample', scatter_dimension=1, tiled=True)  53.1 us
    psum x1, blocking collectives, shards(): lax.psum((jnp.sum(forward * forward), jnp.sum(gradient * gradient)), ('sa...  39.8 us
    gather x4, local copies, waits for them, and re-layouts, pick_buses(): jnp.take(wind_piece, jnp.clip(bus_ids, 0, piece_width - 1), axis=1)  20.7 us
    dot_general x1, matrix products, shards(): lax.dot_general(wind_piece, ptdf, (((1,), (1,)), ((), ())), preferred_ele...  17.1 us
    unnamed x28, local copies, waits for them, and re-layouts  15.8 us
    reduce_scatter x1, waiting for transfers between devices, shards(): lax.psum_scatter(gradient_part, 'sample', scatter_dimension=1, tiled=True)  15.7 us
    dot_general x1, matrix products, penalty_terms(): lax.dot_general(outer_prod, curve_term, (((0,), (0,)), ((), ())), precisi...  9.38 us
  transfers between devices with their start and end apart: 3, of which 3 were waited for; matrix products, arithmetic and copies ran while one was open for 8% of the time, Pallas kernels for 0%

commit v1 on v0

--- a/solution.py
+++ b/solution.py
@@ -110,7 +110,8 @@
         )
         return jnp.where(inside[None, :], picked, 0.0)
 
-    wind_piece = lax.all_gather(wind_dev, "line", axis=1, tiled=True)
+    sent = jnp.stack([wind_dev] * lax.axis_size("line"))
+    wind_piece = jnp.concatenate(lax.all_to_all(sent, "line", 0, 0), axis=1)
     grid_flow = lax.dot_general(
         wind_piece, ptdf, (((1,), (1,)), ((), ())), preferred_element_type=jnp.float32
     )

time: 438 us -> 491 us (1.12)
  waiting for transfers between devices: 237 us -> 277 us
  starting transfers between devices: 0.12 us -> 6.52 us
  local copies, waits for them, and re-layouts: 53.6 us -> 59.9 us
    all_to_all x0 -> x1, waiting for transfers between devices: none -> 207 us  [shards(): wind_piece = jnp.concatenate(lax.all_to_all(sent, 'line', 0, 0), axis=1)]
    all_gather x1 -> x0, waiting for transfers between devices: 167 us -> none  [shards(): wind_piece = lax.all_gather(wind_dev, 'line', axis=1, tiled=True)]
    unnamed x28 -> x27, local copies, waits for them, and re-layouts: 15.8 us -> 4.33 us
    reshape x0 -> x1, local copies, waits for them, and re-layouts: none -> 11.5 us  [shards(): wind_piece = jnp.concatenate(lax.all_to_all(sent, 'line', 0, 0), axis=1)]
    all_to_all x0 -> x1, starting transfers between devices: none -> 6.48 us  [shards(): wind_piece = jnp.concatenate(lax.all_to_all(sent, 'line', 0, 0), axis=1)]
    another operation x0 -> x1, local copies, waits for them, and re-layouts: none -> 6.32 us  [shards(): sent = jnp.stack([wind_dev] * lax.axis_size('line'))]
  transfers between devices with their start and end apart: 3 -> 3, of which waited for: 3 -> 3; matrix products, arithmetic and copies ran while one was open for 8% -> 7% of each run, Pallas kernels for 0% -> 0%
where the time goes in v1:
time: 491 us; the launch traced here: 490 us
  waiting for transfers between devices  277 us (56%)
  local copies, waits for them, and re-layouts  59.9 us (12%)
  blocking collectives  49 us (10%)
  matrix products  47.4 us (10%)
  other arithmetic  28.4 us (6%)
  between operations  18.8 us (4%)
  starting transfers between devices  6.52 us (1%)
    all_to_all x1, waiting for transfers between devices, shards(): wind_piece = jnp.concatenate(lax.all_to_all(sent, 'line', 0, 0), axis=1)  207 us
    reduce_scatter x1, waiting for transfers between devices, shards(): lax.psum_scatter(hessian_part, 'sample', scatter_dimension=1, tiled=True)  53.1 us
    psum x1, blocking collectives, shards(): lax.psum((jnp.sum(forward * forward), jnp.sum(gradient * gradient)), ('sa...  39.8 us
    gather x4, local copies, waits for them, and re-layouts, pick_buses(): jnp.take(wind_piece, jnp.clip(bus_ids, 0, piece_width - 1), axis=1)  20.7 us
    dot_general x1, matrix products, shards(): lax.dot_general(wind_piece, ptdf, (((1,), (1,)), ((), ())), preferred_ele...  17.1 us
    reduce_scatter x1, waiting for transfers between devices, shards(): lax.psum_scatter(gradient_part, 'sample', scatter_dimension=1, tiled=True)  16.6 us
    reshape x1, local copies, waits for them, and re-layouts, shards(): wind_piece = jnp.concatenate(lax.all_to_all(sent, 'line', 0, 0), axis=1)  11.5 us
  transfers between devices with their start and end apart: 3, of which 3 were waited for; matrix products, arithmetic and copies ran while one was open for 7% of the time, Pallas kernels for 0%

profile of v1, /device:TPU:0, one launch (start us, length us, event | category | flops | bytes accessed | tf_op | source)
XLA Modules:
  0.0 490.2 jit_solution(4977183389038718477)
XLA Ops:
  7.2 6.3 %stack.2 = bf16[4,512,2500]{1,2,0:T(8,128)(2,1)} broadcast(bf16[512,2500]{0,1:T(8,128)(2,1)} %param.17), dimensions={1,2} | broadcast | bytes 12800000 | tf_op jit(solution)/shard_map/stack | solution.py:113
  13.5 6.5 %all-to-all-start = ((bf16[4,512,2500]{1,2,0:T(8,128)(2,1)}), bf16[4,512,2500]{1,2,0:T(8,128)(2,1)}, u32[]{:S(2)}, u32[]{:S(2)}) async-start(bf16[4,512,2500]{1,2,0:T(8,128)(2,1)} %stack.2), calls=%async_computation | async-start | bytes 20512768 | tf_op jit(solution)/shard_map/all_to_all | solution.py:114
  20.0 4.3 copy.16
  24.3 5.7 %gather_fusion = s32[1024,2]{1,0:T(8,128)S(1)} fusion(s32[12706,2]{1,0:T(8,128)} %copy.16, s32[1024]{0:T(1024)S(1)} %fusion.32), kind=kCustom, calls=%fused_computation.2 | custom fusion | bytes 20480 | tf_op jit(solution)/shard_map/jit(_take)/gather | solution.py:98
  30.0 6.2 %gather_fusion.1 = f32[1024]{0:T(1024)S(1)} fusion(f32[12706]{0:T(1024)S(1)} %copy-done.2, s32[1024]{0:T(1024)S(1)} %fusion.32), kind=kCustom, calls=%fused_computation.3 | custom fusion | bytes 12288 | tf_op jit(solution)/shard_map/jit(_take)/gather | solution.py:101
  36.2 0.2 broadcast_select_fusion.1
  36.4 0.5 clamp_reduce_fusion.1
  36.9 0.5 and_reduce_fusion.1
  37.4 207.0 %all-to-all-done = bf16[4,512,2500]{1,2,0:T(8,128)(2,1)} async-done(((bf16[4,512,2500]{1,2,0:T(8,128)(2,1)}), bf16[4,512,2500]{1,2,0:T(8,128)(2,1)}, u32[]{:S(2)}, u32[]{:S(2)}) %all-to-all-start) | async-done | bytes 10240032 | tf_op jit(solution)/shard_map/all_to_all | solution.py:114
  244.5 11.5 %reshape.169 = bf16[512,10000]{0,1:T(8,128)(2,1)} reshape(bf16[512,4,2500]{0,2,1:T(8,128)(2,1)} %bitcast) | data formatting | bytes 20480000 | tf_op jit(solution)/shard_map/reshape | solution.py:114
  255.9 9.2 %gather_fusion.3 = bf16[1024,512]{1,0:T(8,128)(2,1)S(1)} fusion(bf16[512,10000]{0,1:T(8,128)(2,1)} %reshape.169, s32[1024]{0:T(1024)S(1)} %get-tuple-element.493), kind=kCustom, calls=%fused_computation.1.clone | custom fusion | bytes 2101248 | tf_op jit(solution)/shard_map/jit(_take)/gather | solution.py:108
  265.1 0.5 copy.18
  265.7 9.6 %gather_fusion.2 = bf16[1024,512]{1,0:T(8,128)(2,1)S(1)} fusion(bf16[512,10000]{0,1:T(8,128)(2,1)} %reshape.169, s32[1024]{0:T(1024)S(1)} %get-tuple-element.492), kind=kCustom, calls=%fused_computation.clone | custom fusion | bytes 2101248 | tf_op jit(solution)/shard_map/jit(_take)/gather | solution.py:108
  275.3 1.3 copy.17
  276.6 5.7 %fusion.37 = f32[512,31]{0,1:T(8,128)S(1)} fusion(bf16[512,10000]{0,1:T(8,128)(2,1)} %reshape.169, bf16[31,10000]{1,0:T(8,128)(2,1)S(1)} %copy-done), kind=kOutput, calls=%fused_computation.90 | convolution fusion | flops 317440000 | bytes 10923488 | tf_op jit(solution)/shard_map/dot_general | solution.py:120
  282.3 17.1 %fusion.38 = f32[512,1024]{1,0:T(8,128)S(1)} fusion(bf16[512,10000]{0,1:T(8,128)(2,1)} %reshape.169, bf16[1024,10000]{0,1:T(8,128)(2,1)} %param.18), kind=kOutput, calls=%fused_computation.91 | convolution fusion | flops 10485760000 | bytes 32817152 | tf_op jit(solution)/shard_map/dot_general | solution.py:115
  299.4 4.3 multiply_reduce_fusion.2
  303.8 2.2 fusion.27
  306.0 3.3 fusion.25
  309.2 0.3 broadcast_multiply_fusion
  309.5 0.7 maximum_multiply_fusion
  310.4 1.5 mul.325
  311.9 1.7 dot_general.30
  313.6 9.4 %fusion.23 = f32[31,31,1024]{2,1,0:T(8,128)S(1)} fusion(f32[31,31,512]{2,1,0:T(8,128)S(1)} %dot_general.30, f32[512,1024]{1,0:T(8,128)} %copy-done.12, f32[1024]{0:T(1024)S(1)} %get-tuple-element.484), kind=kOutput, calls=%fused_computation.49 | convolution fusion | flops 6055002112 | bytes 8005632 | tf_op jit(solution)/shard_map/dot_general | solution.py:18
  323.0 0.9 maximum_maximum_fusion
  323.9 2.4 bitcast_multiply_fusion.1
  326.4 16.6 %reduce-scatter.3.cloned.1.call-done = f32[32,128]{1,0:T(8,128)} async-done(((f32[32,1024]{1,0:T(8,128)}), f32[32,128]{1,0:T(8,128)}) %reduce-scatter.3.cloned.1.call-update) | async-done | bytes 16400 | tf_op jit(solution)/shard_map/reduce_scatter | solution.py:139
  343.0 1.3 multiply_reduce_fusion.4
  344.3 53.1 %reduce-scatter.5.cloned.1.call-done = f32[1024,128]{1,0:T(8,128)} async-done(((f32[1024,1024]{1,0:T(8,128)}), f32[1024,128]{1,0:T(8,128)}) %reduce-scatter.5.cloned.1.call-update) | async-done | bytes 524304 | tf_op jit(solution)/shard_map/reduce_scatter | solution.py:138
  397.4 1.2 multiply_add_fusion.5
  398.7 15.0 %while.51 = (s32[]{:T(128)}, f32[32,32,128]{2,1,0:T(8,128)S(1)}, f32[32,32,128]{2,1,0:T(8,128)S(1)}, s32[]{:T(128)}, s32[]{:T(128)}) while((s32[]{:T(128)}, f32[32,32,128]{2,1,0:T(8,128)S(1)}, f32[32,32,128]{2,1,0:T(8,128)S(1)}, s32[]{:T(128)}, s32[]{:T(128)}) %tuple.129), condition=%wide.region_4.6_spmd.clone.clone, body=%wide.region_2.5_spmd.clone.clone.sunk | while | flops 925923 | bytes 2787745 | solution.py:50
  399.0 0.1 multiply_add_fusion.12
  399.5 0.1 multiply_add_fusion.12
  400.0 0.1 multiply_add_fusion.12
  400.4 0.1 multiply_add_fusion.12
  400.9 0.1 multiply_add_fusion.12
  401.4 0.1 multiply_add_fusion.12
  401.8 0.1 multiply_add_fusion.12
  402.3 0.1 multiply_add_fusion.12
  402.8 0.1 multiply_add_fusion.12
  403.2 0.1 multiply_add_fusion.12
  403.7 0.1 multiply_add_fusion.12
  404.2 0.1 multiply_add_fusion.12
  404.7 0.1 multiply_add_fusion.12
  405.1 0.1 multiply_add_fusion.12
  405.6 0.1 multiply_add_fusion.12
  406.1 0.1 multiply_add_fusion.12
  406.5 0.1 multiply_add_fusion.12
  407.0 0.1 multiply_add_fusion.12
  407.5 0.1 multiply_add_fusion.12
  408.4 0.1 multiply_add_fusion.12
  408.9 0.1 multiply_add_fusion.12
  409.8 0.1 multiply_add_fusion.12
  410.3 0.1 multiply_add_fusion.12
  411.2 0.1 multiply_add_fusion.12
  411.7 0.1 multiply_add_fusion.12
  413.1 0.1 multiply_add_fusion.12
  413.7 4.2 while.49
  417.9 0.6 multiply_reduce_fusion.5
  418.5 5.2 %while.50 = (s32[]{:T(128)}, f32[32,128]{1,0:T(8,128)S(1)}, f32[32,128]{1,0:T(8,128)S(1)}, f32[32,32,128]{2,1,0:T(8,128)S(1)}, s32[]{:T(128)}, /*index=5*/s32[]{:T(128)}, s32[]{:T(128)}, s32[]{:T(128)}) while((s32[]{:T(128)}, f32[32,128]{1,0:T(8,128)S(1)}, f32[32,128]{1,0:T(8,128)S(1)}, f32[32,32,128]{2,1,0:T(8,128)S(1)}, ...), condition=%wide.region_14.16_spmd.clone, body=%wide.region_12.15_spmd.clone.sunk | while | flops 24776 | bytes 101814 | solution.py:73
  423.7 9.2 %all_gather.3 = f32[32,1024]{1,0:T(8,128)S(1)} all-gather(f32[32,128]{1,0:T(8,128)S(1)} %neg.15), channel_id=1, replica_groups=mesh['sample'=8,'line'=4] {'sample'}, dimensions={1}, use_global_device_ids=true | all-gather | bytes 147456 | tf_op jit(solution)/shard_map/all_gather | solution.py:149
  433.0 39.8 %all-reduce = (f32[]{:T(128)}, f32[]{:T(128)}) all-reduce(f32[]{:T(128)} %multiply_reduce_fusion.5, f32[]{:T(128)} %get-tuple-element.482), channel_id=1, replica_groups=mesh['sample'=8,'line'=4] {'sample','line'}, use_global_device_ids=true, to_apply=%region_11.13 | all-reduce | flops 2 | bytes 16 | tf_op jit(solution)/shard_map/psum | solution.py:146
  474.2 0.7 multiply_add_fusion.6
  474.9 5.5 %multiply_add_fusion.3 = f32[512,1024]{1,0:T(8,128)} fusion(f32[512,1024]{1,0:T(8,128)} %copy-done.12, f32[512,31]{0,1:T(8,128)S(1)} %fusion.37, f32[1024]{0:T(1024)S(1)} %bitcast.135, f32[]{:T(128)S(6)} %div.86, f32[32,1024]{1,0:T(8,128)S(1)} %all_gather.3, bf16[1024,512]{0,1:T(8,128)(2,1)S(1)} %copy-done.4, pred[1024]{0:T(1024)(128)(4,1)S(1)} %get-tuple-element.490, ...), kind=kOutput, calls=%fused_computation.51 | convolution fusion | flops 200802304 | bytes 6494212 | tf_op jit(solution)/shard_map/dot_general | solution.py:155
  (561 shorter events, 17.8 us)
Async XLA Ops:
  7.2 269.5 %copy-start = (bf16[31,10000]{1,0:T(8,128)(2,1)S(1)}, bf16[31,10000]{1,0:T(8,128)(2,1)}, u32[]{:S(2)}) copy-start(bf16[31,10000]{1,0:T(8,128)(2,1)} %param.19) | copy-start | bytes 1860004
  13.5 6.5 %copy-start.8 = (s32[12706,2]{0,1:T(2,128)S(1)}, s32[12706,2]{0,1:T(2,128)}, u32[]{:S(2)}) copy-start(s32[12706,2]{0,1:T(2,128)} %param.20) | copy-start | bytes 304948
  13.5 230.9 %all-to-all-start = ((bf16[4,512,2500]{1,2,0:T(8,128)(2,1)}), bf16[4,512,2500]{1,2,0:T(8,128)(2,1)}, u32[]{:S(2)}, u32[]{:S(2)}) async-start(bf16[4,512,2500]{1,2,0:T(8,128)(2,1)} %stack.2), calls=%async_computation | async-start | bytes 20512768 | tf_op jit(solution)/shard_map/all_to_all | solution.py:114
  20.0 4.3 copy-start.9
  20.0 323.0 %reduce-scatter.3.cloned.1.call-start = ((), (), s32[]{:S(2)}) async-start(), calls=%async_computation.3 | async-start | bytes 147456 | tf_op jit(solution)/shard_map/reduce_scatter | solution.py:139
  24.3 5.7 %copy-start.2 = (f32[12706]{0:T(1024)S(1)}, f32[12706]{0:T(1024)}, u32[]{:S(2)}) copy-start(f32[12706]{0:T(1024)} %param.22) | copy-start | bytes 152476
  29.9 6.2 %copy-start.7 = (f32[32,1024]{1,0:T(8,128)S(1)}, f32[32,1024]{1,0:T(8,128)}, u32[]{:S(2)}) copy-start(f32[32,1024]{1,0:T(8,128)} %param.25) | copy-start | bytes 393220
  36.1 1.3 copy-start.10
  265.7 40.3 %copy-start.3 = (bf16[1024,512]{0,1:T(8,128)(2,1)}, bf16[1024,512]{0,1:T(8,128)(2,1)S(1)}, u32[]{:S(2)}) copy-start(bf16[1024,512]{0,1:T(8,128)(2,1)S(1)} %copy.18) | copy-start | bytes 3145732
  282.3 17.1 %copy-start.5 = (bf16[1024,512]{0,1:T(8,128)(2,1)S(1)}, bf16[1024,512]{0,1:T(8,128)(2,1)}, u32[]{:S(2)}) copy-start(bf16[1024,512]{0,1:T(8,128)(2,1)} %copy.17) | copy-start | bytes 3145732
  282.3 17.1 %copy-start.11 = (f32[1024]{0:T(1024)S(1)}, f32[1024]{0:T(1024)}, u32[]{:S(2)}) copy-start(f32[1024]{0:T(1024)} %param.23) | copy-start | bytes 12292
  303.7 2.2 copy-start.12
  310.2 87.2 %reduce-scatter.5.cloned.1.call-start = ((), (), s32[]{:S(2)}) async-start(), calls=%async_computation.4 | async-start | bytes 4718592 | tf_op jit(solution)/shard_map/reduce_scatter | solution.py:138
  398.7 76.2 %copy-start.4 = (bf16[1024,512]{0,1:T(8,128)(2,1)S(1)}, bf16[1024,512]{0,1:T(8,128)(2,1)}, u32[]{:S(2)}) copy-start(bf16[1024,512]{0,1:T(8,128)(2,1)} %copy-done.3) | copy-start | bytes 3145732
  398.7 76.2 %copy-start.6 = (bf16[1024,512]{0,1:T(8,128)(2,1)S(1)}, bf16[1024,512]{0,1:T(8,128)(2,1)}, u32[]{:S(2)}) copy-start(bf16[1024,512]{0,1:T(8,128)(2,1)} %copy.17) | copy-start | bytes 3145732
  474.9 6.3 %copy-start.1 = (bf16[31,10000]{1,0:T(8,128)(2,1)S(1)}, bf16[31,10000]{1,0:T(8,128)(2,1)}, u32[]{:S(2)}) copy-start(bf16[31,10000]{1,0:T(8,128)(2,1)} %param.19) | copy-start | bytes 1860004
Sparse Core Ops, SparseCore 0:
  310.3 32.6 reduce-scatter.2
  346.3 51.0 reduce-scatter.4
